TPU v7x, 512 devices: a whole 4x8x8 slice. The times are simulated.
512 devices in a mesh: section: 32 (over x, y_hi, core), dp: 16 (over y_lo, z).
Axes of the slice: x: 4, y: 8 (y_hi: 4, y_lo: 2; y = y_hi * 2 + y_lo), z: 8, core: 2. Of those that a mesh axis runs over, the one named last changes fastest.
Arguments:
- out_pair: float32 [2048, 2048], P('dp'), may hold values from -6 to 6
- out_grad: bfloat16 [2048, 2048], P('dp'), may hold values from -6 to 6
- f_weight: bfloat16 [32, 1024, 1024], P('section', 'dp'), may hold values from -0.09375 to 0.09375
- g_weight: bfloat16 [32, 1024, 1024], P('section', 'dp'), may hold values from -0.09375 to 0.09375
- gains: float32 [32, 2, 1024], P('section'), may hold values from 0.1 to 1.9
Outputs:
- in_pair: float32 [32, 2048, 2048], P('section', 'dp')
- in_grad: bfloat16 [32, 2048, 2048], P('section', 'dp')
- f_grad: float32 [32, 1024, 1024], P('section', 'dp')
- g_grad: float32 [32, 1024, 1024], P('section', 'dp')
- gains_grad: float32 [32, 2, 1024], P('section')
All inputs are finite; a program needn't handle non-finite values.
Results may differ from a plain program's by a relative error of at most 0.04.
Values may be sent and summed in bfloat16 or wider, within the bound.
A program may use at most 64 MiB of HBM per device.

v0:
```python
import functools

import jax
import jax.numpy as jnp
from jax import lax
from jax.experimental import pallas as pl
from jax.experimental.pallas import tpu as pltpu
from jax.sharding import PartitionSpec as P

offset = 0.25
MESH = pl.DeviceIdType.MESH
f32, bf16 = jnp.float32, jnp.bfloat16


def silu_parts(pre_values):
    sigmoid_value = jax.nn.sigmoid(pre_values)
    return (pre_values * sigmoid_value, sigmoid_value * (1.0 + pre_values * (1.0 - sigmoid_value)))


def inverse_scale(values):
    return lax.rsqrt(jnp.mean(values * values, axis=-1, keepdims=True) + offset)


def kernel(
    n, sections, blocks,
    pair_ref, grad_ref, fw_ref, gw_ref, gains_ref,
    in_pair_ref, in_grad_ref, f_out, g_out, gain_out,
    wf, wg, wft, wgt, aside, rx, tx, held, slopes, norms_own, norms, deltas, gain_parts,
    own_sem, i_send, i_recv, h_send, h_recv, o_send, o_recv, w_send, w_recv, p_send, p_recv, n_send, n_recv, d_send, d_recv, c_send, c_recv,
):
    s, d = lax.axis_index("section"), lax.axis_index("dp")
    is_last = s == sections - 1
    has_below = s > 0
    not_last = jnp.logical_not(is_last)
    tokens = pair_ref.shape[0]
    h = pair_ref.shape[1] // 2
    part = fw_ref.shape[0]
    rows_per = tokens // blocks

    def peer(k):
        return lax.rem(d + k, n)

    barrier = pltpu.get_barrier_semaphore()
    for k in range(1, n):
        pl.semaphore_signal(barrier, inc=1, device_id=(s, peer(k)), device_id_type=MESH)

    @pl.when(has_below)
    def _():
        pl.semaphore_signal(barrier, inc=1, device_id=(s - 1, d), device_id_type=MESH)

    @pl.when(not_last)
    def _():
        pl.semaphore_signal(barrier, inc=1, device_id=(s + 1, d), device_id_type=MESH)

    half = sections // 2
    partner = lax.rem(s + half, sections)
    high, low = s >= half, s < half
    pl.semaphore_signal(barrier, inc=1, device_id=(partner, d), device_id_type=MESH)
    neighbours = n + has_below.astype(jnp.int32) + not_last.astype(jnp.int32)
    pl.semaphore_wait(barrier, neighbours)

    fulls, owns, turned = (wg, wf), (gw_ref, fw_ref), (wgt, wft)
    keep = h - aside.shape[3]
    variants = ((low, pl.ds(0, h)), (high, pl.ds(0, keep)))
    rest = pl.ds(keep, h - keep)

    def shard(a, owner, cols):
        return fulls[a].at[pl.ds(pl.multiple_of(owner * part, part), part), cols]

    def owner_of(way, k):
        return d - k if way == 0 else d + k

    def ahead(way):
        return d + 1 if way == 0 else d - 1

    def hop(a, way, k, cols):
        owner = owner_of(way, k)
        src = owns[a].at[:, cols] if k == 0 else shard(a, owner, cols)
        return pltpu.make_async_remote_copy(
            src_ref=src, dst_ref=shard(a, owner, cols),
            send_sem=w_send.at[a, way, k], recv_sem=w_recv.at[a, way, k],
            device_id=(s, ahead(way)), device_id_type=MESH,
        )

    def aside_in(a):
        return pltpu.make_async_remote_copy(
            src_ref=owns[a].at[:, rest], dst_ref=aside.at[a, d],
            send_sem=i_send.at[a], recv_sem=i_recv.at[a],
            device_id=(partner, d), device_id_type=MESH,
        )

    def aside_hop(a, way, k):
        owner = owner_of(way, k)
        return pltpu.make_async_remote_copy(
            src_ref=aside.at[a, owner], dst_ref=aside.at[a, owner],
            send_sem=h_send.at[a, way, k], recv_sem=h_recv.at[a, way, k],
            device_id=(s, ahead(way)), device_id_type=MESH,
        )

    def aside_out(a, way, k):
        owner = owner_of(way, k)
        return pltpu.make_async_remote_copy(
            src_ref=aside.at[a, owner], dst_ref=shard(a, owner, rest),
            send_sem=o_send.at[a, way, k], recv_sem=o_recv.at[a, way, k],
            device_id=(partner, d), device_id_type=MESH,
        )

    def wait_bytes(ref, sem):
        pltpu.make_async_copy(ref, ref, sem).wait()

    def reach(way, k):
        if way == 0:
            return jnp.logical_and(d - k >= 0, d < n - 1)
        return jnp.logical_and(d + k < n, d > 0)

    def arrives(way, k):
        return d - k >= 0 if way == 0 else d + k < n

    both = jnp.logical_and

    @pl.when(high)
    def _():
        for a in range(2):
            aside_in(a).start()

    @pl.when(low)
    def _():
        for a in range(2):
            wait_bytes(aside.at[a, d], i_recv.at[a])
            for way in range(2):
                @pl.when(reach(way, 0))
                def _():
                    aside_hop(a, way, 0).start()

    for a in range(2):
        for way in range(2):
            for side, cols in variants:
                @pl.when(both(side, reach(way, 0)))
                def _():
                    hop(a, way, 0, cols).start()
    early = part % 128 == 0

    def turn(a, owner):
        span = pl.ds(pl.multiple_of(owner * part, part), part)
        turned[a][:, span] = fulls[a][span, :].T

    own_copies = [
        pltpu.make_async_copy(owns[a], shard(a, d, pl.ds(0, h)), own_sem.at[a]) for a in range(2)
    ]
    for copy in own_copies:
        copy.start()
    for a, copy in enumerate(own_copies):
        copy.wait()
        if early:
            turn(a, d)
    for k in range(1, n):
        for a in range(2):
            for way in range(2):
                @pl.when(both(low, arrives(way, k)))
                def _():
                    wait_bytes(aside.at[a, owner_of(way, k)], h_recv.at[a, way, k - 1])
                    if k < n - 1:
                        @pl.when(reach(way, k))
                        def _():
                            aside_hop(a, way, k).start()
                    aside_out(a, way, k).start()
        for a in range(2):
            for way in range(2):
                for side, cols in variants:
                    @pl.when(both(side, arrives(way, k)))
                    def _():
                        wait_bytes(shard(a, owner_of(way, k), cols), w_recv.at[a, way, k - 1])

                    if k < n - 1:
                        @pl.when(both(side, reach(way, k)))
                        def _():
                            hop(a, way, k, cols).start()
        for a in range(2):
            for way in range(2):
                @pl.when(both(high, arrives(way, k)))
                def _():
                    wait_bytes(shard(a, owner_of(way, k), rest), o_recv.at[a, way, k])

                if early:
                    @pl.when(arrives(way, k))
                    def _():
                        turn(a, owner_of(way, k))
    if not early:
        for a in range(2):
            turned[a][...] = fulls[a][...].T

    gain_out[...] = jnp.zeros_like(gain_out)

    def pair_copy(i, b):
        rows = pl.ds(pl.multiple_of(b * rows_per, rows_per), rows_per)
        return pltpu.make_async_remote_copy(
            src_ref=tx.at[i, rows], dst_ref=rx.at[i, rows],
            send_sem=p_send.at[i], recv_sem=p_recv.at[i, b],
            device_id=(s - 1, d), device_id_type=MESH,
        )

    def take(i, b, rows, source, column):
        @pl.when(is_last)
        def _():
            held[i] = source[rows, column].astype(f32)

        @pl.when(not_last)
        def _():
            rows_ = pl.ds(pl.multiple_of(b * rows_per, rows_per), rows_per)
            pltpu.make_async_remote_copy(
                src_ref=tx.at[i, rows_], dst_ref=rx.at[i, rows_],
                send_sem=p_send.at[i], recv_sem=p_recv.at[i, b],
                device_id=(s + 1, d), device_id_type=MESH,
            ).wait_recv()
            held[i] = rx[i, rows].astype(f32)

    def give(i, b, rows, values):
        tx[i, rows] = values.astype(bf16)

        @pl.when(has_below)
        def _():
            pair_copy(i, b).start()

    def share_norm(a, rows, normed):
        for e in range(n):
            norms_own[a, e, rows] = normed[:, e * part:(e + 1) * part]
        for k in range(1, n):
            e = peer(k)
            pltpu.make_async_remote_copy(
                src_ref=norms_own.at[a, e, rows], dst_ref=norms.at[a, d, rows],
                send_sem=n_send.at[a], recv_sem=n_recv.at[a],
                device_id=(s, e), device_id_type=MESH,
            ).start()

    def delta_hop(a, way, k, rows):
        owner = d - k if way == 0 else d + k
        return pltpu.make_async_remote_copy(
            src_ref=deltas.at[a, owner, rows], dst_ref=deltas.at[a, owner, rows],
            send_sem=d_send.at[a, way, k], recv_sem=d_recv.at[a, way, k],
            device_id=(s, d + 1 if way == 0 else d - 1), device_id_type=MESH,
        )

    def share_delta(a, rows, delta):
        deltas[a, d, rows] = delta
        for way in range(2):
            @pl.when(reach(way, 0))
            def _():
                delta_hop(a, way, 0, rows).start()

    first, second = pl.ds(0, h), pl.ds(h, h)

    def block(b, carry):
        rows = pl.ds(pl.multiple_of(b * rows_per, rows_per), rows_per)
        gain_f, gain_g = gains_ref[0:1, :], gains_ref[1:2, :]
        take(0, b, rows, pair_ref, first)
        y1 = held[0]
        r1 = inverse_scale(y1)
        norm_g = (y1 * r1 * gain_g).astype(bf16)
        pre_g = jnp.dot(norm_g, wg[...], preferred_element_type=f32)
        take(1, b, rows, pair_ref, second)
        act_g, slope_g = silu_parts(pre_g)
        x2 = held[1] - act_g
        in_pair_ref[rows, second] = x2
        give(1, b, rows, x2)
        slopes[0] = slope_g
        r2 = inverse_scale(x2)
        norm_f = (x2 * r2 * gain_f).astype(bf16)
        pre_f = jnp.dot(norm_f, wf[...], preferred_element_type=f32)
        act_f, slope_f = silu_parts(pre_f)
        x1 = held[0] - act_f
        in_pair_ref[rows, first] = x1
        give(0, b, rows, x1)
        slopes[1] = slope_f
        share_norm(0, rows, norm_f)
        share_norm(1, rows, norm_g)

        take(3, b, rows, grad_ref, second)
        take(2, b, rows, grad_ref, first)
        delta_g = (held[3] * slopes[0]).astype(bf16)
        back_g = jnp.dot(delta_g, wgt[...], preferred_element_type=f32)
        share_delta(1, rows, delta_g)
        y1 = held[0]
        weighted = gain_g * back_g
        gz = held[2] + r1 * weighted - y1 * (r1 * r1 * r1) * jnp.mean(
            weighted * y1, axis=-1, keepdims=True
        )
        in_grad_ref[rows, first] = gz.astype(bf16)
        give(2, b, rows, gz)
        gain_out[1:2, :] += jnp.sum(back_g * y1 * r1, axis=0, keepdims=True)
        delta_f = (gz * slopes[1]).astype(bf16)
        back_f = jnp.dot(delta_f, wft[...], preferred_element_type=f32)
        share_delta(0, rows, delta_f)
        x2 = in_pair_ref[rows, second]
        weighted = gain_f * back_f
        gx2 = held[3] + r2 * weighted - x2 * (r2 * r2 * r2) * jnp.mean(
            weighted * x2, axis=-1, keepdims=True
        )
        in_grad_ref[rows, second] = gx2.astype(bf16)
        give(3, b, rows, gx2)
        gain_out[0:1, :] += jnp.sum(back_f * x2 * r2, axis=0, keepdims=True)
        return carry

    lax.fori_loop(0, blocks, block, 0)

    gain_parts[d] = gain_out[...]
    for k in range(1, n):
        pltpu.make_async_remote_copy(
            src_ref=gain_parts.at[d], dst_ref=gain_parts.at[d],
            send_sem=c_send, recv_sem=c_recv,
            device_id=(s, peer(k)), device_id_type=MESH,
        ).start()

    for a in range(2):
        norms[a, d] = norms_own[a, d]
    others, whole = pl.ds(0, n - 1), pl.ds(0, tokens)
    for k in range(1, n):
        for a, out in ((1, g_out), (0, f_out)):
            for way in range(2):
                @pl.when(arrives(way, k))
                def _():
                    wait_bytes(deltas.at[a, d - k if way == 0 else d + k], d_recv.at[a, way, k - 1])

                if k < n - 1:
                    @pl.when(reach(way, k))
                    def _():
                        delta_hop(a, way, k, whole).start()
            if k == n - 1:
                wait_bytes(norms.at[a, others], n_recv.at[a])
                out[...] = lax.dot_general(
                    norms[a].reshape(n * tokens, part), deltas[a].reshape(n * tokens, h),
                    (((0,), (0,)), ((), ())), preferred_element_type=f32,
                )
    wait_bytes(gain_parts.at[others], c_recv)
    total = gain_parts[0]
    for e in range(1, n):
        total = total + gain_parts[e]
    gain_out[...] = total

    for a in range(2):
        wait_bytes(norms.at[a, others], n_send.at[a])
        for k in range(n - 1):
            for way in range(2):
                @pl.when(reach(way, k))
                def _():
                    wait_bytes(deltas.at[a, d - k if way == 0 else d + k], d_send.at[a, way, k])
    wait_bytes(gain_parts.at[others], c_send)

    @pl.when(has_below)
    def _():
        for i in range(4):
            wait_bytes(tx.at[i], p_send.at[i])

    @pl.when(high)
    def _():
        for a in range(2):
            aside_in(a).wait_send()

    for k in range(n):
        for a in range(2):
            for way in range(2):
                if k < n - 1:
                    for side, cols in variants:
                        @pl.when(both(side, reach(way, k)))
                        def _():
                            hop(a, way, k, cols).wait_send()

                    @pl.when(both(low, reach(way, k)))
                    def _():
                        aside_hop(a, way, k).wait_send()
                if k > 0:
                    @pl.when(both(low, arrives(way, k)))
                    def _():
                        aside_out(a, way, k).wait_send()


def shards(out_pair, out_grad, f_weight, g_weight, gains):
    n, sections = lax.axis_size("dp"), lax.axis_size("section")
    tokens, width = out_pair.shape
    h = width // 2
    part = f_weight.shape[1]
    blocks = 4
    vmem = pl.BlockSpec(memory_space=pltpu.VMEM)
    dma = pltpu.SemaphoreType.DMA
    outs = pl.pallas_call(
        functools.partial(kernel, n, sections, blocks),
        out_shape=(
            jax.ShapeDtypeStruct((tokens, width), f32),
            jax.ShapeDtypeStruct((tokens, width), bf16),
            jax.ShapeDtypeStruct((part, h), f32),
            jax.ShapeDtypeStruct((part, h), f32),
            jax.ShapeDtypeStruct((2, h), f32),
        ),
        in_specs=[vmem] * 5,
        out_specs=[vmem] * 5,
        scratch_shapes=[
            pltpu.VMEM((h, h), bf16),
            pltpu.VMEM((h, h), bf16),
            pltpu.VMEM((h, h), bf16),
            pltpu.VMEM((h, h), bf16),
            pltpu.VMEM((2, n, part, h // 8), bf16),
            pltpu.VMEM((4, tokens, h), bf16),
            pltpu.VMEM((4, tokens, h), bf16),
            pltpu.VMEM((4, tokens // blocks, h), f32),
            pltpu.VMEM((2, tokens // blocks, h), f32),
            pltpu.VMEM((2, n, tokens, part), bf16),
            pltpu.VMEM((2, n, tokens, part), bf16),
            pltpu.VMEM((2, n, tokens, h), bf16),
            pltpu.VMEM((n, 2, h), f32),
            dma((2,)),
            dma((2,)),
            dma((2,)),
            dma((2, 2, n)),
            dma((2, 2, n)),
            dma((2, 2, n)),
            dma((2, 2, n)),
            dma((2, 2, n)),
            dma((2, 2, n)),
            dma((4,)),
            dma((4, blocks)),
            dma((2,)),
            dma((2,)),
            dma((2, 2, n)),
            dma((2, 2, n)),
            dma,
            dma,
        ],
        compiler_params=pltpu.CompilerParams(
            collective_id=0, has_side_effects=True, vmem_limit_bytes=60 * 1024 * 1024
        ),
    )(out_pair, out_grad, f_weight[0], g_weight[0], gains[0])
    return tuple(out[None] for out in outs)


def solution(mesh):
    placed = (
        P("dp", None),
        P("dp", None),
        P("section", "dp", None),
        P("section", "dp", None),
        P("section", None, None),
    )
    return jax.shard_map(
        shards,
        mesh=mesh,
        in_specs=placed,
        out_specs=(
            P("section", "dp", None),
            P("section", "dp", None),
            P("section", "dp", None),
            P("section", "dp", None),
            P("section", None, None),
        ),
        check_vma=False,
    )
```

profile of v0, /device:TPU:1, one launch (start us, length us, event | category | flops | bytes accessed | tf_op | source)
XLA Modules:
  0.0 437.4 jit_solution(1697950079731416626)
XLA Ops:
  0.6 431.0 %shard_map.92 = (f32[128,2048]{1,0:T(8,128)}, bf16[128,2048]{1,0:T(8,128)(2,1)}, f32[64,1024]{1,0:T(8,128)}, f32[64,1024]{1,0:T(8,128)}, f32[2,1024]{1,0:T(2,128)}) custom-call(f32[128,2048]{1,0:T(8,128)} %pair_ref.1, bf16[128,2048]{1,0:T(8,128)(2,1)} %grad_ref.1, bf16[64,1024]{1,0:T(8,128)(2,1)} %bitcast.12, bf16[64,1024]{1,0:T(8,128)(2,1)} %bitcast.13, ...), custom_call_target="tpu_custom_call" | custom-call | tf_op jit(solution)/shard_map/pallas_call | solution.py:384
  431.6 0.0 copy-start
  431.6 2.4 copy.15
  434.0 0.0 copy-done
  434.0 0.0 copy-start.2
  434.0 0.8 copy.16
  434.8 0.3 copy-done.2
  435.1 0.0 copy-start.1
  435.1 0.7 copy.17
  435.8 0.3 copy-done.1
  436.1 0.0 copy-start.3
  436.1 0.7 copy.18
  436.8 0.0 copy-done.3
  436.8 0.6 copy.19
Async XLA Ops:
  431.6 2.4 copy-start
  434.0 1.1 copy-start.2
  435.1 1.0 copy-start.1
  436.1 0.7 copy-start.3
where the time goes:
time: 438 us; the launch traced here: 437 us
  Pallas kernels  431 us (98%)
  local copies, waits for them, and re-layouts  5.8 us (1%)
    pallas_call x1, Pallas kernels, shards(): pl.pallas_call(functools.partial(kernel, n, sections, blocks), out_shape=...  431 us

commit v1 on v0

v1 whole, which is shorter than its diff:
```python
import functools

import jax
import jax.numpy as jnp
from jax import lax
from jax.experimental import pallas as pl
from jax.experimental.pallas import tpu as pltpu
from jax.sharding import PartitionSpec as P

offset = 0.25
MESH = pl.DeviceIdType.MESH
f32, bf16 = jnp.float32, jnp.bfloat16


def kernel(
    n, sections, blocks,
    pair_ref, grad_ref, fw_ref, gw_ref, gains_ref,
    in_pair_ref, in_grad_ref, f_out, g_out, gain_out,
    wf, wg, wft, wgt, rx, tx, y1s, pres, slopes, norm_full, norm_cat, delta_cat, sums, rs_rx, rs_tx, gain_parts,
    own_sem, zs, zr, os_, or_, ys, yr, y2s, y2r, p_send, p_recv, n_send, n_recv, d_send, d_recv, r_send, r_recv, c_send, c_recv,
):
    s, d = lax.axis_index("section"), lax.axis_index("dp")
    is_last = s == sections - 1
    has_below = s > 0
    not_last = jnp.logical_not(is_last)
    tokens = pair_ref.shape[0]
    h = pair_ref.shape[1] // 2
    part = fw_ref.shape[0]
    rows_per = tokens // blocks
    zn = n // 2
    hh = zn * part
    z, row = lax.rem(d, zn), d // zn
    beside = (1 - row) * zn + z
    ring_next = (row * zn + lax.rem(z + 1, zn), row * zn + lax.rem(z + zn - 1, zn))

    barrier = pltpu.get_barrier_semaphore()
    for k in range(1, n):
        pl.semaphore_signal(barrier, inc=1, device_id=(s, lax.rem(d + k, n)), device_id_type=MESH)

    @pl.when(has_below)
    def _():
        pl.semaphore_signal(barrier, inc=1, device_id=(s - 1, d), device_id_type=MESH)

    @pl.when(not_last)
    def _():
        pl.semaphore_signal(barrier, inc=1, device_id=(s + 1, d), device_id_type=MESH)

    pl.semaphore_wait(barrier, n - 1 + has_below.astype(jnp.int32) + not_last.astype(jnp.int32))

    def remote(src, dst, send, recv, target):
        return pltpu.make_async_remote_copy(
            src_ref=src, dst_ref=dst, send_sem=send, recv_sem=recv,
            device_id=target, device_id_type=MESH,
        )

    def wait_bytes(ref, sem):
        pltpu.make_async_copy(ref, ref, sem).wait()

    fulls, owns, turned = (wg, wf), (gw_ref, fw_ref), (wgt, wft)
    c1 = h * 5 // 8
    cols_1, cols_2, all_cols = pl.ds(0, c1), pl.ds(c1, h - c1), pl.ds(0, h)
    reach = ((zn // 2, zn - 1 - zn // 2), (zn - 1 - zn // 2, zn // 2))

    def ring_pos(way, k):
        return lax.rem(z + (zn - k if way == 0 else k), zn)

    def shard(a, line, pos, cols):
        return fulls[a].at[pl.ds(pl.multiple_of((line * zn + pos) * part, part), part), cols]

    def own_hop(a, way, k):
        dst = shard(a, row, ring_pos(way, k), all_cols)
        return remote(owns[a] if k == 0 else dst, dst, zs.at[a, way, k], zr.at[a, way, k], (s, ring_next[way]))

    def other_hop(a, way, k):
        ref = shard(a, 1 - row, ring_pos(way, k), cols_2)
        return remote(ref, ref, os_.at[a, way, k], or_.at[a, way, k], (s, ring_next[way]))

    def cross(a, way, k):
        dst = shard(a, row, ring_pos(way, k), cols_1)
        return remote(owns[a].at[:, cols_1] if k == 0 else dst, dst, ys.at[a, way, k], yr.at[a, way, k], (s, beside))

    def cross_2(a):
        return remote(owns[a].at[:, cols_2], shard(a, row, z, cols_2), y2s.at[a], y2r.at[a], (s, beside))

    own_copies = [pltpu.make_async_copy(owns[a], shard(a, row, z, all_cols), own_sem.at[a]) for a in range(2)]
    for a in range(2):
        cross_2(a).start()
        for way in range(2):
            own_hop(a, way, 0).start()
        cross(a, 0, 0).start()
        own_copies[a].start()

    parity = lax.rem(z, 2)
    pairs = zn // 2

    def turn(a, line, step):
        shift = (0, 2 * parity - 1, 1 - 2 * parity, 2)[step]
        chunk = line * pairs + lax.rem(z // 2 + shift + pairs, pairs)
        span = pl.ds(pl.multiple_of(chunk * 2 * part, 2 * part), 2 * part)
        turned[a][:, span] = fulls[a][span, :].T

    def take_cross(a, k):
        for way in range(2):
            if (k > 0 or way == 0) and k <= reach[a][way]:
                wait_bytes(shard(a, 1 - row, ring_pos(way, k), cols_1), yr.at[a, way, k])

    for a in range(2):
        wait_bytes(shard(a, 1 - row, z, cols_2), y2r.at[a])
        for way in range(2):
            other_hop(a, way, 0).start()
    for a in range(2):
        own_copies[a].wait()

    for k in range(1, pairs + 1):
        for a in range(2):
            for way in range(2):
                if k <= reach[a][way]:
                    wait_bytes(shard(a, row, ring_pos(way, k), all_cols), zr.at[a, way, k - 1])
                    if k < reach[a][way]:
                        own_hop(a, way, k).start()
                    cross(a, way, k).start()
            for way in range(2):
                if k <= reach[a][way]:
                    wait_bytes(shard(a, 1 - row, ring_pos(way, k), cols_2), or_.at[a, way, k - 1])
                    if k < reach[a][way]:
                        other_hop(a, way, k).start()
        for a in range(2):
            take_cross(a, k - 1)
            turn(a, row, k - 1)
            if k > 1:
                turn(a, 1 - row, k - 2)
    for a in range(2):
        take_cross(a, pairs)
        turn(a, 1 - row, pairs - 1)

    gain_out[...] = jnp.zeros_like(gain_out)

    def incoming(i, b):
        return pl.ds(pl.multiple_of(b * rows_per, rows_per), rows_per)

    def await_from_above(i, b):
        @pl.when(not_last)
        def _():
            wait_bytes(rx.at[i, incoming(i, b)], p_recv.at[i, b])

    def give(i, b, rows, values):
        tx[i, rows] = values.astype(bf16)

        @pl.when(has_below)
        def _():
            remote(tx.at[i, rows], rx.at[i, rows], p_send.at[i], p_recv.at[i, b], (s - 1, d)).start()

    def share_norm(a, b, rows, normed):
        norm_full[a, rows] = normed
        remote(
            norm_full.at[a, rows, pl.ds(pl.multiple_of((1 - row) * hh, hh), hh)], norm_cat.at[a, 1, rows],
            n_send.at[a], n_recv.at[a], (s, beside),
        ).start()

    def share_delta(a, b, rows):
        remote(
            delta_cat.at[a, 0, rows], delta_cat.at[a, 1, rows],
            d_send.at[a], d_recv.at[a], (s, beside),
        ).start()

    first, second = pl.ds(0, h), pl.ds(h, h)

    def scale_of(values):
        return lax.rsqrt(jnp.sum(values * values, axis=-1, keepdims=True) * (1.0 / h) + offset)

    def block(b, carry):
        rows = pl.ds(pl.multiple_of(b * rows_per, rows_per), rows_per)
        gain_f, gain_g = gains_ref[0:1, :], gains_ref[1:2, :]
        await_from_above(1, b)
        await_from_above(0, b)
        y1 = jnp.where(is_last, pair_ref[rows, first], rx[0, rows].astype(f32))
        y2 = jnp.where(is_last, pair_ref[rows, second], rx[1, rows].astype(f32))
        y1s[...] = y1
        r1 = scale_of(y1)
        pre_g = jnp.dot((y1 * gain_g).astype(bf16), wg[...], preferred_element_type=f32) * r1
        sig_g = jax.nn.sigmoid(pre_g)
        x2 = y2 - pre_g * sig_g
        give(1, b, rows, x2)
        r2 = scale_of(x2)
        pre_f = jnp.dot((x2 * gain_f).astype(bf16), wf[...], preferred_element_type=f32) * r2
        sig_f = jax.nn.sigmoid(pre_f)
        x1 = y1 - pre_f * sig_f
        give(0, b, rows, x1)
        in_pair_ref[rows, first] = x1
        in_pair_ref[rows, second] = x2
        pres[0] = pre_g
        pres[1] = pre_f
        slopes[0] = sig_g * (1.0 + pre_g * (1.0 - sig_g))
        slopes[1] = sig_f * (1.0 + pre_f * (1.0 - sig_f))
        share_norm(0, b, rows, (y1 * r1 * gain_g).astype(bf16))
        share_norm(1, b, rows, (x2 * r2 * gain_f).astype(bf16))

        await_from_above(2, b)
        await_from_above(3, b)
        gy1 = jnp.where(is_last, grad_ref[rows, first].astype(f32), rx[2, rows].astype(f32))
        gy2 = jnp.where(is_last, grad_ref[rows, second].astype(f32), rx[3, rows].astype(f32))
        delta_g = (gy2 * slopes[0]).astype(bf16)
        back_g = jnp.dot(delta_g, wgt[...], preferred_element_type=f32)
        mean_g = jnp.sum(delta_g.astype(f32) * pres[0], axis=-1, keepdims=True) * (1.0 / h)
        y1 = y1s[...]
        gz = gy1 + (r1 * gain_g) * back_g - y1 * (mean_g * (r1 * r1))
        give(2, b, rows, gz)
        delta_f = (gz * slopes[1]).astype(bf16)
        back_f = jnp.dot(delta_f, wft[...], preferred_element_type=f32)
        mean_f = jnp.sum(delta_f.astype(f32) * pres[1], axis=-1, keepdims=True) * (1.0 / h)
        x2 = in_pair_ref[rows, second]
        gx2 = gy2 + (r2 * gain_f) * back_f - x2 * (mean_f * (r2 * r2))
        give(3, b, rows, gx2)
        in_grad_ref[rows, first] = gz.astype(bf16)
        in_grad_ref[rows, second] = gx2.astype(bf16)
        delta_cat[0, 0, rows] = delta_g
        delta_cat[1, 0, rows] = delta_f
        share_delta(0, b, rows)
        share_delta(1, b, rows)
        gain_out[1:2, :] += jnp.sum(back_g * (y1 * r1), axis=0, keepdims=True)
        gain_out[0:1, :] += jnp.sum(back_f * (x2 * r2), axis=0, keepdims=True)
        return carry

    lax.fori_loop(0, blocks, block, 0)

    gain_parts[d] = gain_out[...]
    for k in range(1, n):
        remote(gain_parts.at[d], gain_parts.at[d], c_send, c_recv, (s, lax.rem(d + k, n))).start()

    for a in range(2):
        norm_cat[a, 0] = norm_full[a, :, pl.ds(pl.multiple_of(row * hh, hh), hh)]

    def slot(pos):
        return pl.ds(pl.multiple_of(pos * part, part), part)

    def sum_hop(a, way, t):
        return remote(rs_tx.at[a, way, t], rs_rx.at[a, way, t], r_send.at[a, way, t], r_recv.at[a, way, t], (s, ring_next[way]))

    def sum_pos(a, way, t):
        far = reach[a][way] - t
        return lax.rem(z + (far if way == 0 else zn - far), zn)

    for a in range(2):
        wait_bytes(norm_cat.at[a, 1], n_recv.at[a])
        wait_bytes(delta_cat.at[a, 1], d_recv.at[a])
        sums[a] = lax.dot_general(
            norm_cat[a].reshape(2 * tokens, hh), delta_cat[a].reshape(2 * tokens, h),
            (((0,), (0,)), ((), ())), preferred_element_type=f32,
        )
        for way in range(2):
            if reach[a][way] > 0:
                rs_tx[a, way, 0] = sums[a, slot(sum_pos(a, way, 0))].astype(bf16)
                sum_hop(a, way, 0).start()
    for t in range(1, pairs):
        for a in range(2):
            for way in range(2):
                if t < reach[a][way]:
                    wait_bytes(rs_rx.at[a, way, t - 1], r_recv.at[a, way, t - 1])
                    rs_tx[a, way, t] = (sums[a, slot(sum_pos(a, way, t))] + rs_rx[a, way, t - 1].astype(f32)).astype(bf16)
                    sum_hop(a, way, t).start()
    for a, out in ((0, g_out), (1, f_out)):
        total = sums[a, slot(z)]
        for way in range(2):
            if reach[a][way] > 0:
                last = reach[a][way] - 1
                wait_bytes(rs_rx.at[a, way, last], r_recv.at[a, way, last])
                total = total + rs_rx[a, way, last].astype(f32)
        out[...] = total

    others = pl.ds(0, n - 1)
    wait_bytes(gain_parts.at[others], c_recv)
    total = gain_parts[0]
    for e in range(1, n):
        total = total + gain_parts[e]
    gain_out[...] = total

    wait_bytes(gain_parts.at[others], c_send)
    for a in range(2):
        wait_bytes(norm_cat.at[a, 1], n_send.at[a])
        wait_bytes(delta_cat.at[a, 1], d_send.at[a])
        cross_2(a).wait_send()
        cross(a, 0, 0).wait_send()
        for way in range(2):
            for k in range(reach[a][way]):
                own_hop(a, way, k).wait_send()
                other_hop(a, way, k).wait_send()
                cross(a, way, k + 1).wait_send()
                sum_hop(a, way, k).wait_send()

    @pl.when(has_below)
    def _():
        for i in range(4):
            wait_bytes(tx.at[i], p_send.at[i])


def shards(out_pair, out_grad, f_weight, g_weight, gains):
    n, sections = lax.axis_size("dp"), lax.axis_size("section")
    tokens, width = out_pair.shape
    h = width // 2
    part = f_weight.shape[1]
    blocks = 4
    zn = n // 2
    hops = max(zn // 2, 1)
    rows_per = tokens // blocks
    vmem = pl.BlockSpec(memory_space=pltpu.VMEM)
    dma = pltpu.SemaphoreType.DMA
    outs = pl.pallas_call(
        functools.partial(kernel, n, sections, blocks),
        out_shape=(
            jax.ShapeDtypeStruct((tokens, width), f32),
            jax.ShapeDtypeStruct((tokens, width), bf16),
            jax.ShapeDtypeStruct((part, h), f32),
            jax.ShapeDtypeStruct((part, h), f32),
            jax.ShapeDtypeStruct((2, h), f32),
        ),
        in_specs=[vmem] * 5,
        out_specs=[vmem] * 5,
        scratch_shapes=[
            pltpu.VMEM((h, h), bf16),
            pltpu.VMEM((h, h), bf16),
            pltpu.VMEM((h, h), bf16),
            pltpu.VMEM((h, h), bf16),
            pltpu.VMEM((4, tokens, h), bf16),
            pltpu.VMEM((4, tokens, h), bf16),
            pltpu.VMEM((rows_per, h), f32),
            pltpu.VMEM((2, rows_per, h), f32),
            pltpu.VMEM((2, rows_per, h), f32),
            pltpu.VMEM((2, tokens, h), bf16),
            pltpu.VMEM((2, 2, tokens, zn * part), bf16),
            pltpu.VMEM((2, 2, tokens, h), bf16),
            pltpu.VMEM((2, zn * part, h), f32),
            pltpu.VMEM((2, 2, hops, part, h), bf16),
            pltpu.VMEM((2, 2, hops, part, h), bf16),
            pltpu.VMEM((n, 2, h), f32),
            dma((2,)),
            dma((2, 2, hops)),
            dma((2, 2, hops)),
            dma((2, 2, hops)),
            dma((2, 2, hops)),
            dma((2, 2, hops + 1)),
            dma((2, 2, hops + 1)),
            dma((2,)),
            dma((2,)),
            dma((4,)),
            dma((4, blocks)),
            dma((2,)),
            dma((2,)),
            dma((2,)),
            dma((2,)),
            dma((2, 2, hops)),
            dma((2, 2, hops)),
            dma,
            dma,
        ],
        compiler_params=pltpu.CompilerParams(
            collective_id=0, has_side_effects=True, vmem_limit_bytes=60 * 1024 * 1024
        ),
    )(out_pair, out_grad, f_weight[0], g_weight[0], gains[0])
    return tuple(out[None] for out in outs)


def solution(mesh):
    placed = (
        P("dp", None),
        P("dp", None),
        P("section", "dp", None),
        P("section", "dp", None),
        P("section", None, None),
    )
    return jax.shard_map(
        shards,
        mesh=mesh,
        in_specs=placed,
        out_specs=(
            P("section", "dp", None),
            P("section", "dp", None),
            P("section", "dp", None),
            P("section", "dp", None),
            P("section", None, None),
        ),
        check_vma=False,
    )
```

time: 438 us -> 246 us (0.56)
  Pallas kernels: 431 us -> 238 us
    pallas_call x1, Pallas kernels: 431 us -> 238 us  [shards(): pl.pallas_call(functools.partial(kernel, n, sections, blocks), out_shape=...]
where the time goes in v1:
time: 246 us; the launch traced here: 244 us
  Pallas kernels  238 us (97%)
  local copies, waits for them, and re-layouts  5.8 us (2%)
    pallas_call x1, Pallas kernels, shards(): pl.pallas_call(functools.partial(kernel, n, sections, blocks), out_shape=...  238 us
    unnamed x13, local copies, waits for them, and re-layouts  5.8 us

profile of v1, /device:TPU:1, one launch (start us, length us, event | category | flops | bytes accessed | tf_op | source)
XLA Modules:
  0.0 244.2 jit_solution(16050676107888913172)
XLA Ops:
  0.6 237.8 %shard_map.92 = (f32[128,2048]{1,0:T(8,128)}, bf16[128,2048]{1,0:T(8,128)(2,1)}, f32[64,1024]{1,0:T(8,128)}, f32[64,1024]{1,0:T(8,128)}, f32[2,1024]{1,0:T(2,128)}) custom-call(f32[128,2048]{1,0:T(8,128)} %pair_ref.1, bf16[128,2048]{1,0:T(8,128)(2,1)} %grad_ref.1, bf16[64,1024]{1,0:T(8,128)(2,1)} %bitcast.12, bf16[64,1024]{1,0:T(8,128)(2,1)} %bitcast.13, ...), custom_call_target="tpu_custom_call" | custom-call | tf_op jit(solution)/shard_map/pallas_call | solution.py:307
  238.4 0.0 copy-start
  238.4 2.4 copy.15
  240.8 0.0 copy-done
  240.8 0.0 copy-start.2
  240.8 0.8 copy.16
  241.6 0.3 copy-done.2
  241.9 0.0 copy-start.1
  241.9 0.7 copy.17
  242.6 0.3 copy-done.1
  242.9 0.0 copy-start.3
  242.9 0.7 copy.18
  243.6 0.0 copy-done.3
  243.6 0.6 copy.19
Async XLA Ops:
  238.4 2.4 copy-start
  240.8 1.1 copy-start.2
  241.9 1.0 copy-start.1
  242.9 0.7 copy-start.3

commit v2 on v1

--- a/solution.py
+++ b/solution.py
@@ -17,7 +17,7 @@
     pair_ref, grad_ref, fw_ref, gw_ref, gains_ref,
     in_pair_ref, in_grad_ref, f_out, g_out, gain_out,
     wf, wg, wft, wgt, rx, tx, y1s, pres, slopes, norm_full, norm_cat, delta_cat, sums, rs_rx, rs_tx, gain_parts,
-    own_sem, zs, zr, os_, or_, ys, yr, y2s, y2r, p_send, p_recv, n_send, n_recv, d_send, d_recv, r_send, r_recv, c_send, c_recv,
+    own_sem, zs, zr, os_, or_, ys, yr, y2s, y2r, p_send, p_recv, n_send, n_recv, d_send, d_recv, r_send, r_recv, c_send, c_recv, turn_sem,
 ):
     s, d = lax.axis_index("section"), lax.axis_index("dp")
     is_last = s == sections - 1
@@ -150,32 +150,51 @@
         def _():
             remote(tx.at[i, rows], rx.at[i, rows], p_send.at[i], p_recv.at[i, b], (s - 1, d)).start()
 
+    early = s < 2
+
+    def norm_copy(a, rows):
+        return remote(
+            norm_full.at[a, rows, pl.ds(pl.multiple_of((1 - row) * hh, hh), hh)], norm_cat.at[a, 1, rows],
+            n_send.at[a], n_recv.at[a], (s, beside),
+        )
+
+    def delta_copy(a, rows):
+        return remote(
+            delta_cat.at[a, 0, rows], delta_cat.at[a, 1, rows],
+            d_send.at[a], d_recv.at[a], (s, beside),
+        )
+
     def share_norm(a, b, rows, normed):
         norm_full[a, rows] = normed
-        remote(
-            norm_full.at[a, rows, pl.ds(pl.multiple_of((1 - row) * hh, hh), hh)], norm_cat.at[a, 1, rows],
-            n_send.at[a], n_recv.at[a], (s, beside),
-        ).start()
+
+        @pl.when(early)
+        def _():
+            norm_copy(a, rows).start()
 
     def share_delta(a, b, rows):
-        remote(
-            delta_cat.at[a, 0, rows], delta_cat.at[a, 1, rows],
-            d_send.at[a], d_recv.at[a], (s, beside),
-        ).start()
+        @pl.when(early)
+        def _():
+            delta_copy(a, rows).start()
 
     first, second = pl.ds(0, h), pl.ds(h, h)
 
     def scale_of(values):
         return lax.rsqrt(jnp.sum(values * values, axis=-1, keepdims=True) * (1.0 / h) + offset)
 
-    def block(b, carry):
+    def pace(here):
+        @pl.when(here)
+        def _():
+            pl.delay(1000)
+
+    def upper_half(b, carry):
         rows = pl.ds(pl.multiple_of(b * rows_per, rows_per), rows_per)
         gain_f, gain_g = gains_ref[0:1, :], gains_ref[1:2, :]
+        pace(jnp.logical_and(is_last, b > 0))
         await_from_above(1, b)
         await_from_above(0, b)
         y1 = jnp.where(is_last, pair_ref[rows, first], rx[0, rows].astype(f32))
         y2 = jnp.where(is_last, pair_ref[rows, second], rx[1, rows].astype(f32))
-        y1s[...] = y1
+        y1s[rows] = y1
         r1 = scale_of(y1)
         pre_g = jnp.dot((y1 * gain_g).astype(bf16), wg[...], preferred_element_type=f32) * r1
         sig_g = jax.nn.sigmoid(pre_g)
@@ -188,27 +207,35 @@
         give(0, b, rows, x1)
         in_pair_ref[rows, first] = x1
         in_pair_ref[rows, second] = x2
-        pres[0] = pre_g
-        pres[1] = pre_f
-        slopes[0] = sig_g * (1.0 + pre_g * (1.0 - sig_g))
-        slopes[1] = sig_f * (1.0 + pre_f * (1.0 - sig_f))
+        pres[0, rows] = pre_g
+        pres[1, rows] = pre_f
+        slopes[0, rows] = sig_g * (1.0 + pre_g * (1.0 - sig_g))
+        slopes[1, rows] = sig_f * (1.0 + pre_f * (1.0 - sig_f))
         share_norm(0, b, rows, (y1 * r1 * gain_g).astype(bf16))
         share_norm(1, b, rows, (x2 * r2 * gain_f).astype(bf16))
 
+        return carry
+
+    def lower_half(b, carry):
+        rows = pl.ds(pl.multiple_of(b * rows_per, rows_per), rows_per)
+        gain_f, gain_g = gains_ref[0:1, :], gains_ref[1:2, :]
+        pace(is_last)
         await_from_above(2, b)
         await_from_above(3, b)
         gy1 = jnp.where(is_last, grad_ref[rows, first].astype(f32), rx[2, rows].astype(f32))
         gy2 = jnp.where(is_last, grad_ref[rows, second].astype(f32), rx[3, rows].astype(f32))
-        delta_g = (gy2 * slopes[0]).astype(bf16)
+        delta_g = (gy2 * slopes[0, rows]).astype(bf16)
         back_g = jnp.dot(delta_g, wgt[...], preferred_element_type=f32)
-        mean_g = jnp.sum(delta_g.astype(f32) * pres[0], axis=-1, keepdims=True) * (1.0 / h)
-        y1 = y1s[...]
+        mean_g = jnp.sum(delta_g.astype(f32) * pres[0, rows], axis=-1, keepdims=True) * (1.0 / h)
+        y1 = y1s[rows]
+        r1 = scale_of(y1)
         gz = gy1 + (r1 * gain_g) * back_g - y1 * (mean_g * (r1 * r1))
         give(2, b, rows, gz)
-        delta_f = (gz * slopes[1]).astype(bf16)
+        delta_f = (gz * slopes[1, rows]).astype(bf16)
         back_f = jnp.dot(delta_f, wft[...], preferred_element_type=f32)
-        mean_f = jnp.sum(delta_f.astype(f32) * pres[1], axis=-1, keepdims=True) * (1.0 / h)
+        mean_f = jnp.sum(delta_f.astype(f32) * pres[1, rows], axis=-1, keepdims=True) * (1.0 / h)
         x2 = in_pair_ref[rows, second]
+        r2 = scale_of(x2)
         gx2 = gy2 + (r2 * gain_f) * back_f - x2 * (mean_f * (r2 * r2))
         give(3, b, rows, gx2)
         in_grad_ref[rows, first] = gz.astype(bf16)
@@ -221,7 +248,29 @@
         gain_out[0:1, :] += jnp.sum(back_f * (x2 * r2), axis=0, keepdims=True)
         return carry
 
-    lax.fori_loop(0, blocks, block, 0)
+    lax.fori_loop(0, blocks, upper_half, 0)
+    lax.fori_loop(0, blocks, lower_half, 0)
+
+    @pl.when(has_below)
+    def _():
+        for i in range(4):
+            wait_bytes(tx.at[i], p_send.at[i])
+
+    upper = lax.rem(s, 2) == 1
+
+    @pl.when(jnp.logical_not(early))
+    def _():
+        @pl.when(jnp.logical_not(upper))
+        def _():
+            pl.semaphore_signal(turn_sem, inc=1, device_id=(s + 1, d), device_id_type=MESH)
+
+        @pl.when(upper)
+        def _():
+            pl.semaphore_wait(turn_sem, 1)
+
+        for a in range(2):
+            norm_copy(a, pl.ds(0, tokens)).start()
+            delta_copy(a, pl.ds(0, tokens)).start()
 
     gain_parts[d] = gain_out[...]
     for k in range(1, n):
@@ -287,10 +336,19 @@
                 cross(a, way, k + 1).wait_send()
                 sum_hop(a, way, k).wait_send()
 
-    @pl.when(has_below)
-    def _():
-        for i in range(4):
-            wait_bytes(tx.at[i], p_send.at[i])
+
+def hand_over(*refs):
+    n = (len(refs) - 2) // 3
+    ins, outs, held, in_sem, out_sem = refs[:n], refs[n:2 * n], refs[2 * n:3 * n], refs[-2], refs[-1]
+    loads = [pltpu.make_async_copy(ins[i], held[i], in_sem.at[i]) for i in range(n)]
+    stores = [pltpu.make_async_copy(held[i], outs[i].at[0], out_sem.at[i]) for i in range(n)]
+    for copy in loads:
+        copy.start()
+    for load, store in zip(loads, stores):
+        load.wait()
+        store.start()
+    for copy in stores:
+        copy.wait()
 
 
 def shards(out_pair, out_grad, f_weight, g_weight, gains):
@@ -298,10 +356,9 @@
     tokens, width = out_pair.shape
     h = width // 2
     part = f_weight.shape[1]
-    blocks = 4
+    blocks = 8
     zn = n // 2
     hops = max(zn // 2, 1)
-    rows_per = tokens // blocks
     vmem = pl.BlockSpec(memory_space=pltpu.VMEM)
     dma = pltpu.SemaphoreType.DMA
     outs = pl.pallas_call(
@@ -322,9 +379,9 @@
             pltpu.VMEM((h, h), bf16),
             pltpu.VMEM((4, tokens, h), bf16),
             pltpu.VMEM((4, tokens, h), bf16),
-            pltpu.VMEM((rows_per, h), f32),
-            pltpu.VMEM((2, rows_per, h), f32),
-            pltpu.VMEM((2, rows_per, h), f32),
+            pltpu.VMEM((tokens, h), f32),
+            pltpu.VMEM((2, tokens, h), f32),
+            pltpu.VMEM((2, tokens, h), f32),
             pltpu.VMEM((2, tokens, h), bf16),
             pltpu.VMEM((2, 2, tokens, zn * part), bf16),
             pltpu.VMEM((2, 2, tokens, h), bf16),
@@ -351,12 +408,20 @@
             dma((2, 2, hops)),
             dma,
             dma,
+            pltpu.SemaphoreType.REGULAR,
         ],
         compiler_params=pltpu.CompilerParams(
             collective_id=0, has_side_effects=True, vmem_limit_bytes=60 * 1024 * 1024
         ),
     )(out_pair, out_grad, f_weight[0], g_weight[0], gains[0])
-    return tuple(out[None] for out in outs)
+    count = len(outs)
+    return pl.pallas_call(
+        hand_over,
+        out_shape=tuple(jax.ShapeDtypeStruct((1,) + out.shape, out.dtype) for out in outs),
+        in_specs=[pl.BlockSpec(memory_space=pl.ANY)] * count,
+        out_specs=tuple([pl.BlockSpec(memory_space=pl.ANY)] * count),
+        scratch_shapes=[pltpu.VMEM(out.shape, out.dtype) for out in outs] + [dma((count,)), dma((count,))],
+    )(*outs)
 
 
 def solution(mesh):

time: 246 us -> 216 us (0.88)
  the two profiles are of different devices: /device:TPU:1 before, /device:TPU:24 now
where the time goes in v2:
time: 216 us
  Pallas kernels  215 us (100%)
    pallas_call x1, Pallas kernels, shards(): pl.pallas_call(functools.partial(kernel, n, sections, blocks), out_shape=...  213 us

profile of v2, /device:TPU:24, one launch (start us, length us, event | category | flops | bytes accessed | tf_op | source)
XLA Modules:
  0.0 216.1 jit_solution(5906642509042503330)
XLA Ops:
  0.6 212.9 %shard_map.92 = (f32[128,2048]{1,0:T(8,128)}, bf16[128,2048]{1,0:T(8,128)(2,1)}, f32[64,1024]{1,0:T(8,128)}, f32[64,1024]{1,0:T(8,128)}, f32[2,1024]{1,0:T(2,128)}) custom-call(f32[128,2048]{1,0:T(8,128)} %pair_ref.1, bf16[128,2048]{1,0:T(8,128)(2,1)} %grad_ref.1, bf16[64,1024]{1,0:T(8,128)(2,1)} %bitcast.3, bf16[64,1024]{1,0:T(8,128)(2,1)} %bitcast.4, ...), custom_call_target="tpu_custom_call" | custom-call | tf_op jit(solution)/shard_map/pallas_call | solution.py:364
  213.5 2.6 %shard_map.93 = (f32[1,128,2048]{2,1,0:T(8,128)}, bf16[1,128,2048]{2,1,0:T(8,128)(2,1)}, f32[1,64,1024]{2,1,0:T(8,128)}, f32[1,64,1024]{2,1,0:T(8,128)}, f32[1,2,1024]{2,1,0:T(2,128)}) custom-call(f32[128,2048]{1,0:T(8,128)} %get-tuple-element.10.refs_0_, bf16[128,2048]{1,0:T(8,128)(2,1)} %get-tuple-element.11.refs_1_, ...), custom_call_target="tpu_custom_call" | custom-call | tf_op jit(solution)/shard_map/pallas_call | solution.py:418

commit v3 on v2

--- a/solution.py
+++ b/solution.py
@@ -13,11 +13,11 @@
 
 
 def kernel(
-    n, sections, blocks,
+    n, sections, blocks, cuts,
     pair_ref, grad_ref, fw_ref, gw_ref, gains_ref,
     in_pair_ref, in_grad_ref, f_out, g_out, gain_out,
-    wf, wg, wft, wgt, rx, tx, y1s, pres, slopes, norm_full, norm_cat, delta_cat, sums, rs_rx, rs_tx, gain_parts,
-    own_sem, zs, zr, os_, or_, ys, yr, y2s, y2r, p_send, p_recv, n_send, n_recv, d_send, d_recv, r_send, r_recv, c_send, c_recv, turn_sem,
+    wf, wg, wft, wgt, rx, tx, y1s, pres, slopes, norm_full, norm_cat, delta_cat, sums, norm_turned, rs_rx, rs_tx, res_tx, res_rx, gain_parts,
+    own_sem, zs, zr, os_, or_, ys, yr, y2s, y2r, p_send, p_recv, n_send, n_recv, d_send, d_recv, r_send, r_recv, c_send, c_recv, turn_sem, nl_send, nl_recv, dl_send, dl_recv, s_send, s_recv,
 ):
     s, d = lax.axis_index("section"), lax.axis_index("dp")
     is_last = s == sections - 1
@@ -45,7 +45,19 @@
     def _():
         pl.semaphore_signal(barrier, inc=1, device_id=(s + 1, d), device_id_type=MESH)
 
-    pl.semaphore_wait(barrier, n - 1 + has_below.astype(jnp.int32) + not_last.astype(jnp.int32))
+    client, proxy = 1, 1 + sections * 3 // 4
+    is_client, is_proxy = s == client, s == proxy
+
+    @pl.when(is_client)
+    def _():
+        pl.semaphore_signal(barrier, inc=1, device_id=(proxy, d), device_id_type=MESH)
+
+    @pl.when(is_proxy)
+    def _():
+        pl.semaphore_signal(barrier, inc=1, device_id=(client, d), device_id_type=MESH)
+
+    linked = jnp.logical_or(is_client, is_proxy).astype(jnp.int32)
+    pl.semaphore_wait(barrier, n - 1 + has_below.astype(jnp.int32) + not_last.astype(jnp.int32) + linked)
 
     def remote(src, dst, send, recv, target):
         return pltpu.make_async_remote_copy(
@@ -150,31 +162,48 @@
         def _():
             remote(tx.at[i, rows], rx.at[i, rows], p_send.at[i], p_recv.at[i, b], (s - 1, d)).start()
 
-    early = s < 2
-
-    def norm_copy(a, rows):
+    streams = jnp.logical_and(s < 4, jnp.logical_not(is_client))
+    away = pl.ds(pl.multiple_of((1 - row) * hh, hh), hh)
+
+    def norm_copy(q, a, rows):
         return remote(
-            norm_full.at[a, rows, pl.ds(pl.multiple_of((1 - row) * hh, hh), hh)], norm_cat.at[a, 1, rows],
-            n_send.at[a], n_recv.at[a], (s, beside),
+            norm_full.at[q, a, rows, away], norm_cat.at[q, a, 1, rows],
+            n_send.at[q, a], n_recv.at[q, a], (s, beside),
         )
 
-    def delta_copy(a, rows):
+    def delta_copy(q, a, rows):
         return remote(
-            delta_cat.at[a, 0, rows], delta_cat.at[a, 1, rows],
-            d_send.at[a], d_recv.at[a], (s, beside),
+            delta_cat.at[q, a, 0, rows], delta_cat.at[q, a, 1, rows],
+            d_send.at[q, a], d_recv.at[q, a], (s, beside),
         )
 
+    def norm_lend(a, b, rows):
+        return remote(norm_full.at[0, a, rows], norm_full.at[1, a, rows], nl_send.at[a], nl_recv.at[a, b], (proxy, d))
+
+    def delta_lend(a, b, rows):
+        return remote(
+            delta_cat.at[0, a, 0, rows], delta_cat.at[1, a, 0, rows], dl_send.at[a], dl_recv.at[a, b], (proxy, d)
+        )
+
     def share_norm(a, b, rows, normed):
-        norm_full[a, rows] = normed
-
-        @pl.when(early)
-        def _():
-            norm_copy(a, rows).start()
+        norm_full[0, a, rows] = normed
+
+        @pl.when(streams)
+        def _():
+            norm_copy(0, a, rows).start()
+
+        @pl.when(is_client)
+        def _():
+            norm_lend(a, b, rows).start()
 
     def share_delta(a, b, rows):
-        @pl.when(early)
-        def _():
-            delta_copy(a, rows).start()
+        @pl.when(streams)
+        def _():
+            delta_copy(0, a, rows).start()
+
+        @pl.when(is_client)
+        def _():
+            delta_lend(a, b, rows).start()
 
     first, second = pl.ds(0, h), pl.ds(h, h)
 
@@ -240,8 +269,8 @@
         give(3, b, rows, gx2)
         in_grad_ref[rows, first] = gz.astype(bf16)
         in_grad_ref[rows, second] = gx2.astype(bf16)
-        delta_cat[0, 0, rows] = delta_g
-        delta_cat[1, 0, rows] = delta_f
+        delta_cat[0, 0, 0, rows] = delta_g
+        delta_cat[0, 1, 0, rows] = delta_f
         share_delta(0, b, rows)
         share_delta(1, b, rows)
         gain_out[1:2, :] += jnp.sum(back_g * (y1 * r1), axis=0, keepdims=True)
@@ -258,7 +287,7 @@
 
     upper = lax.rem(s, 2) == 1
 
-    @pl.when(jnp.logical_not(early))
+    @pl.when(s >= 4)
     def _():
         @pl.when(jnp.logical_not(upper))
         def _():
@@ -269,52 +298,121 @@
             pl.semaphore_wait(turn_sem, 1)
 
         for a in range(2):
-            norm_copy(a, pl.ds(0, tokens)).start()
-            delta_copy(a, pl.ds(0, tokens)).start()
+            norm_copy(0, a, pl.ds(0, tokens)).start()
+            delta_copy(0, a, pl.ds(0, tokens)).start()
 
     gain_parts[d] = gain_out[...]
     for k in range(1, n):
         remote(gain_parts.at[d], gain_parts.at[d], c_send, c_recv, (s, lax.rem(d + k, n))).start()
 
-    for a in range(2):
-        norm_cat[a, 0] = norm_full[a, :, pl.ds(pl.multiple_of(row * hh, hh), hh)]
-
     def slot(pos):
         return pl.ds(pl.multiple_of(pos * part, part), part)
 
-    def sum_hop(a, way, t):
-        return remote(rs_tx.at[a, way, t], rs_rx.at[a, way, t], r_send.at[a, way, t], r_recv.at[a, way, t], (s, ring_next[way]))
+    def sum_hop(q, a, way, t, c):
+        return remote(
+            rs_tx.at[q, a, way, t, c], rs_rx.at[q, a, way, t, c],
+            r_send.at[q, a, way, t, c], r_recv.at[q, a, way, t, c], (s, ring_next[way]),
+        )
+
+    span = h // cuts
+
+    def band(c):
+        return pl.ds(c * span, span)
 
     def sum_pos(a, way, t):
         far = reach[a][way] - t
         return lax.rem(z + (far if way == 0 else zn - far), zn)
 
-    for a in range(2):
-        wait_bytes(norm_cat.at[a, 1], n_recv.at[a])
-        wait_bytes(delta_cat.at[a, 1], d_recv.at[a])
-        sums[a] = lax.dot_general(
-            norm_cat[a].reshape(2 * tokens, hh), delta_cat[a].reshape(2 * tokens, h),
-            (((0,), (0,)), ((), ())), preferred_element_type=f32,
-        )
-        for way in range(2):
-            if reach[a][way] > 0:
-                rs_tx[a, way, 0] = sums[a, slot(sum_pos(a, way, 0))].astype(bf16)
-                sum_hop(a, way, 0).start()
-    for t in range(1, pairs):
-        for a in range(2):
+    def reduce_grads(q, emit):
+        for a in range(2):
+            wait_bytes(norm_cat.at[q, a, 1], n_recv.at[q, a])
+            norm_cat[q, a, 0] = norm_full[q, a, :, pl.ds(pl.multiple_of(row * hh, hh), hh)]
+            norm_turned[a] = norm_cat[q, a].reshape(2 * tokens, hh).T
+        for a in range(2):
+            wait_bytes(delta_cat.at[q, a, 1], d_recv.at[q, a])
+            for c in range(cuts):
+                sums[a, :, band(c)] = jnp.dot(
+                    norm_turned[a], delta_cat[q, a, :, :, band(c)].reshape(2 * tokens, span), preferred_element_type=f32
+                )
+                for way in range(2):
+                    if reach[a][way] > 0:
+                        rs_tx[q, a, way, 0, c] = sums[a, slot(sum_pos(a, way, 0)), band(c)].astype(bf16)
+                        sum_hop(q, a, way, 0, c).start()
+        for t in range(1, pairs):
+            for a in range(2):
+                for c in range(cuts):
+                    for way in range(2):
+                        if t < reach[a][way]:
+                            wait_bytes(rs_rx.at[q, a, way, t - 1, c], r_recv.at[q, a, way, t - 1, c])
+                            rs_tx[q, a, way, t, c] = (
+                                sums[a, slot(sum_pos(a, way, t)), band(c)] + rs_rx[q, a, way, t - 1, c].astype(f32)
+                            ).astype(bf16)
+                            sum_hop(q, a, way, t, c).start()
+        for a in range(2):
+            for c in range(cuts):
+                total = sums[a, slot(z), band(c)]
+                for way in range(2):
+                    if reach[a][way] > 0:
+                        last = reach[a][way] - 1
+                        wait_bytes(rs_rx.at[q, a, way, last, c], r_recv.at[q, a, way, last, c])
+                        total = total + rs_rx[q, a, way, last, c].astype(f32)
+                emit(a, c, total)
+        for a in range(2):
+            wait_bytes(norm_cat.at[q, a, 1], n_send.at[q, a])
+            wait_bytes(delta_cat.at[q, a, 1], d_send.at[q, a])
             for way in range(2):
-                if t < reach[a][way]:
-                    wait_bytes(rs_rx.at[a, way, t - 1], r_recv.at[a, way, t - 1])
-                    rs_tx[a, way, t] = (sums[a, slot(sum_pos(a, way, t))] + rs_rx[a, way, t - 1].astype(f32)).astype(bf16)
-                    sum_hop(a, way, t).start()
-    for a, out in ((0, g_out), (1, f_out)):
-        total = sums[a, slot(z)]
-        for way in range(2):
-            if reach[a][way] > 0:
-                last = reach[a][way] - 1
-                wait_bytes(rs_rx.at[a, way, last], r_recv.at[a, way, last])
-                total = total + rs_rx[a, way, last].astype(f32)
-        out[...] = total
+                for k in range(reach[a][way]):
+                    for c in range(cuts):
+                        sum_hop(q, a, way, k, c).wait_send()
+
+    grads = (g_out, f_out)
+
+    def keep(a, c, total):
+        grads[a][:, band(c)] = total
+
+    def give_back(a, c):
+        return remote(res_tx.at[a, c], res_rx.at[a, c], s_send.at[a, c], s_recv.at[a, c], (client, d))
+
+    def lend_back(a, c, total):
+        res_tx[a, c] = total.astype(bf16)
+        give_back(a, c).start()
+
+    @pl.when(jnp.logical_not(is_client))
+    def _():
+        reduce_grads(0, keep)
+
+    @pl.when(is_proxy)
+    def _():
+        def lent_norms(b, carry):
+            rows = pl.ds(pl.multiple_of(b * rows_per, rows_per), rows_per)
+            for a in range(2):
+                wait_bytes(norm_full.at[1, a, rows], nl_recv.at[a, b])
+                norm_copy(1, a, rows).start()
+            return carry
+
+        def lent_deltas(b, carry):
+            rows = pl.ds(pl.multiple_of(b * rows_per, rows_per), rows_per)
+            for a in range(2):
+                wait_bytes(delta_cat.at[1, a, 0, rows], dl_recv.at[a, b])
+                delta_copy(1, a, rows).start()
+            return carry
+
+        lax.fori_loop(0, blocks, lent_norms, 0)
+        lax.fori_loop(0, blocks, lent_deltas, 0)
+        reduce_grads(1, lend_back)
+        for a in range(2):
+            for c in range(cuts):
+                give_back(a, c).wait_send()
+
+    @pl.when(is_client)
+    def _():
+        for a in range(2):
+            for c in range(cuts):
+                wait_bytes(res_rx.at[a, c], s_recv.at[a, c])
+                grads[a][:, band(c)] = res_rx[a, c].astype(f32)
+        for a in range(2):
+            wait_bytes(norm_full.at[0, a], nl_send.at[a])
+            wait_bytes(delta_cat.at[0, a, 0], dl_send.at[a])
 
     others = pl.ds(0, n - 1)
     wait_bytes(gain_parts.at[others], c_recv)
@@ -325,8 +423,6 @@
 
     wait_bytes(gain_parts.at[others], c_send)
     for a in range(2):
-        wait_bytes(norm_cat.at[a, 1], n_send.at[a])
-        wait_bytes(delta_cat.at[a, 1], d_send.at[a])
         cross_2(a).wait_send()
         cross(a, 0, 0).wait_send()
         for way in range(2):
@@ -334,7 +430,6 @@
                 own_hop(a, way, k).wait_send()
                 other_hop(a, way, k).wait_send()
                 cross(a, way, k + 1).wait_send()
-                sum_hop(a, way, k).wait_send()
 
 
 def hand_over(*refs):
@@ -356,13 +451,13 @@
     tokens, width = out_pair.shape
     h = width // 2
     part = f_weight.shape[1]
-    blocks = 8
+    blocks, cuts = 8, 2
     zn = n // 2
     hops = max(zn // 2, 1)
     vmem = pl.BlockSpec(memory_space=pltpu.VMEM)
     dma = pltpu.SemaphoreType.DMA
     outs = pl.pallas_call(
-        functools.partial(kernel, n, sections, blocks),
+        functools.partial(kernel, n, sections, blocks, cuts),
         out_shape=(
             jax.ShapeDtypeStruct((tokens, width), f32),
             jax.ShapeDtypeStruct((tokens, width), bf16),
@@ -382,12 +477,15 @@
             pltpu.VMEM((tokens, h), f32),
             pltpu.VMEM((2, tokens, h), f32),
             pltpu.VMEM((2, tokens, h), f32),
-            pltpu.VMEM((2, tokens, h), bf16),
-            pltpu.VMEM((2, 2, tokens, zn * part), bf16),
             pltpu.VMEM((2, 2, tokens, h), bf16),
+            pltpu.VMEM((2, 2, 2, tokens, zn * part), bf16),
+            pltpu.VMEM((2, 2, 2, tokens, h), bf16),
             pltpu.VMEM((2, zn * part, h), f32),
-            pltpu.VMEM((2, 2, hops, part, h), bf16),
-            pltpu.VMEM((2, 2, hops, part, h), bf16),
+            pltpu.VMEM((2, zn * part, 2 * tokens), bf16),
+            pltpu.VMEM((2, 2, 2, hops, cuts, part, h // cuts), bf16),
+            pltpu.VMEM((2, 2, 2, hops, cuts, part, h // cuts), bf16),
+            pltpu.VMEM((2, cuts, part, h // cuts), bf16),
+            pltpu.VMEM((2, cuts, part, h // cuts), bf16),
             pltpu.VMEM((n, 2, h), f32),
             dma((2,)),
             dma((2, 2, hops)),
@@ -400,15 +498,21 @@
             dma((2,)),
             dma((4,)),
             dma((4, blocks)),
-            dma((2,)),
-            dma((2,)),
-            dma((2,)),
-            dma((2,)),
-            dma((2, 2, hops)),
-            dma((2, 2, hops)),
+            dma((2, 2)),
+            dma((2, 2)),
+            dma((2, 2)),
+            dma((2, 2)),
+            dma((2, 2, 2, hops, cuts)),
+            dma((2, 2, 2, hops, cuts)),
             dma,
             dma,
             pltpu.SemaphoreType.REGULAR,
+            dma((2,)),
+            dma((2, blocks)),
+            dma((2,)),
+            dma((2, blocks)),
+            dma((2, cuts)),
+            dma((2, cuts)),
         ],
         compiler_params=pltpu.CompilerParams(
             collective_id=0, has_side_effects=True, vmem_limit_bytes=60 * 1024 * 1024

time: 216 us -> 208 us (0.963)
  the two profiles are of different devices: /device:TPU:24 before, /device:TPU:1 now
where the time goes in v3:
time: 208 us
  Pallas kernels  207 us (100%)
    pallas_call x1, Pallas kernels, shards(): pl.pallas_call(functools.partial(kernel, n, sections, blocks, cuts), out_...  204 us

profile of v3, /device:TPU:1, one launch (start us, length us, event | category | flops | bytes accessed | tf_op | source)
XLA Modules:
  0.0 207.7 jit_solution(5921788107308489971)
XLA Ops:
  0.6 204.5 %shard_map.92 = (f32[128,2048]{1,0:T(8,128)}, bf16[128,2048]{1,0:T(8,128)(2,1)}, f32[64,1024]{1,0:T(8,128)}, f32[64,1024]{1,0:T(8,128)}, f32[2,1024]{1,0:T(2,128)}) custom-call(f32[128,2048]{1,0:T(8,128)} %pair_ref.1, bf16[128,2048]{1,0:T(8,128)(2,1)} %grad_ref.1, bf16[64,1024]{1,0:T(8,128)(2,1)} %bitcast.3, bf16[64,1024]{1,0:T(8,128)(2,1)} %bitcast.4, ...), custom_call_target="tpu_custom_call" | custom-call | tf_op jit(solution)/shard_map/pallas_call | solution.py:459
  205.1 2.6 %shard_map.93 = (f32[1,128,2048]{2,1,0:T(8,128)}, bf16[1,128,2048]{2,1,0:T(8,128)(2,1)}, f32[1,64,1024]{2,1,0:T(8,128)}, f32[1,64,1024]{2,1,0:T(8,128)}, f32[1,2,1024]{2,1,0:T(2,128)}) custom-call(f32[128,2048]{1,0:T(8,128)} %get-tuple-element.10.refs_0_, bf16[128,2048]{1,0:T(8,128)(2,1)} %get-tuple-element.11.refs_1_, ...), custom_call_target="tpu_custom_call" | custom-call | tf_op jit(solution)/shard_map/pallas_call | solution.py:522

commit v4 on v3

--- a/solution.py
+++ b/solution.py
@@ -248,7 +248,7 @@
     def lower_half(b, carry):
         rows = pl.ds(pl.multiple_of(b * rows_per, rows_per), rows_per)
         gain_f, gain_g = gains_ref[0:1, :], gains_ref[1:2, :]
-        pace(is_last)
+        pace(jnp.logical_and(is_last, b > 0))
         await_from_above(2, b)
         await_from_above(3, b)
         gy1 = jnp.where(is_last, grad_ref[rows, first].astype(f32), rx[2, rows].astype(f32))

time: 208 us -> 216 us (1.038)
  Pallas kernels: 207 us -> 214 us
    pallas_call x1, Pallas kernels: 204 us -> 211 us  [shards(): pl.pallas_call(functools.partial(kernel, n, sections, blocks, cuts), out_...]
where the time goes in v4:
time: 216 us; the launch traced here: 214 us
  Pallas kernels  214 us (99%)
    pallas_call x1, Pallas kernels, shards(): pl.pallas_call(functools.partial(kernel, n, sections, blocks, cuts), out_...  211 us

profile of v4, /device:TPU:1, one launch (start us, length us, event | category | flops | bytes accessed | tf_op | source)
XLA Modules:
  0.0 214.3 jit_solution(6251784636260278145)
XLA Ops:
  0.6 211.0 %shard_map.92 = (f32[128,2048]{1,0:T(8,128)}, bf16[128,2048]{1,0:T(8,128)(2,1)}, f32[64,1024]{1,0:T(8,128)}, f32[64,1024]{1,0:T(8,128)}, f32[2,1024]{1,0:T(2,128)}) custom-call(f32[128,2048]{1,0:T(8,128)} %pair_ref.1, bf16[128,2048]{1,0:T(8,128)(2,1)} %grad_ref.1, bf16[64,1024]{1,0:T(8,128)(2,1)} %bitcast.3, bf16[64,1024]{1,0:T(8,128)(2,1)} %bitcast.4, ...), custom_call_target="tpu_custom_call" | custom-call | tf_op jit(solution)/shard_map/pallas_call | solution.py:459
  211.7 2.6 %shard_map.93 = (f32[1,128,2048]{2,1,0:T(8,128)}, bf16[1,128,2048]{2,1,0:T(8,128)(2,1)}, f32[1,64,1024]{2,1,0:T(8,128)}, f32[1,64,1024]{2,1,0:T(8,128)}, f32[1,2,1024]{2,1,0:T(2,128)}) custom-call(f32[128,2048]{1,0:T(8,128)} %get-tuple-element.10.refs_0_, bf16[128,2048]{1,0:T(8,128)(2,1)} %get-tuple-element.11.refs_1_, ...), custom_call_target="tpu_custom_call" | custom-call | tf_op jit(solution)/shard_map/pallas_call | solution.py:522
